TPU v7x, 128 devices: a whole 4x4x4 slice. The times are simulated.
128 devices in a mesh: src: 16 (over z, x), rcv: 8 (over y, core).
Axes of the slice: x: 4, y: 4, z: 4, core: 2. Of those that a mesh axis runs over, the one named last changes fastest.
Arguments:
- traces: bfloat16 [2, 2, 2048, 2048], P(None, None, 'src', 'rcv'), may hold values from -8 to 8
- wavelet: float32 [2, 2], replicated, may hold values from -0.3 to 0.3
Outputs:
- coeffs: float32 [2, 2, 2048, 2048], P(None, None, 'src', 'rcv')
- norms: float32 [2, 2], replicated
All inputs are finite; a program needn't handle non-finite values.
Results may differ from a plain program's by a relative error of at most 0.006.
Values may be sent and summed in bfloat16 or wider, within the bound.
A program may use at most 128 MiB of HBM per device.

v0:
```python
import math
import jax
import jax.numpy as jnp
from jax import lax
from jax.sharding import Mesh
from jax.sharding import PartitionSpec as P

ITERS = 2
SRC = ("src_0", "src_1")
RCV = ("rcv_0", "rcv_1")
SRC_RCV = ("src_0", "src_1", "rcv_0", "rcv_1")
step_length = 0.4
shrink_fraction = 0.2


def laid_out(tiles, dim):
    shape = list(tiles.shape[1:])
    shape[dim] *= tiles.shape[0]
    return jnp.moveaxis(tiles, 0, dim).reshape(shape)


def copy_for_each(x, axis):
    copies = jnp.broadcast_to(x, (lax.axis_size(axis), *x.shape))
    return lax.all_to_all(copies, axis, split_axis=0, concat_axis=0, tiled=True)


def gathered_copies(x, axis, dim):
    return laid_out(copy_for_each(x, axis), dim)


def all_in_one(x, axis):
    leaves = jax.tree.leaves(x)
    order = sorted(range(len(leaves)), key=lambda k: -leaves[k].size)
    width = (1, *leaves[order[0]].shape)[-1]
    lines = [
        jnp.pad(leaves[k].reshape(-1), (0, -leaves[k].size % width)).reshape(-1, width)
        for k in order
    ]
    both, at, found = (lax.all_gather(jnp.concatenate(lines), axis), 0, {})
    for k, line in zip(order, lines):
        share = both[:, at : at + len(line)].reshape(len(both), -1)
        found[k] = share[:, : leaves[k].size].reshape(-1, *leaves[k].shape)
        at += len(line)
    numbers = iter(range(len(leaves)))
    return jax.tree.map(lambda _: found[next(numbers)], x)


def once_a_type(x, axis):
    leaves, found = (jax.tree.leaves(x), {})
    for first, a in enumerate(leaves):
        if first not in found:
            alike = [k for k, b in enumerate(leaves) if b.dtype == a.dtype]
            got = (
                all_in_one([leaves[k] for k in alike], axis)
                if len(alike) > 1
                else [lax.all_gather(a, axis)]
            )
            for k, b in zip(alike, got):
                found[k] = b
    numbers = iter(range(len(leaves)))
    return jax.tree.map(lambda _: found[next(numbers)], x)


def joined_all(x, axes, combine):
    for axis in axes:
        pieces = once_a_type(x, axis)
        x = jax.tree.map(lambda part: part[0], pieces)
        for k in range(1, lax.axis_size(axis)):
            x = combine(x, jax.tree.map(lambda part: part[k], pieces))
    return x


def table_block(offset, height, second, breadth, length, direction):
    left_index = offset + jnp.arange(height, dtype=jnp.int32)
    right_index = second + jnp.arange(breadth, dtype=jnp.int32)
    phase = left_index[:, None] * right_index[None, :] % length
    angle = phase.astype(jnp.float32) * (2.0 * math.pi / length)
    scale = 1.0 / math.sqrt(length)
    return jnp.stack([jnp.cos(angle) * scale, direction * (jnp.sin(angle) * scale)]).astype(
        jnp.bfloat16
    )


def complex_product(left_side, right_side, pattern, left_table, right_table):
    left_re = left_side[0] if left_table else left_side[:, 0]
    left_im = left_side[1] if left_table else left_side[:, 1]
    right_re = right_side[0] if right_table else right_side[:, 0]
    right_im = right_side[1] if right_table else right_side[:, 1]

    def single(first_op, second_op):
        return jnp.einsum(pattern, first_op, second_op, preferred_element_type=jnp.float32)

    real_part = single(left_re, right_re) - single(left_im, right_im)
    imag_part = single(left_re, right_im) + single(left_im, right_re)
    return jnp.stack([real_part, imag_part], axis=1)


def complex_scale(real_part, imag_part, values):
    return jnp.stack(
        [
            real_part * values[:, 0] - imag_part * values[:, 1],
            real_part * values[:, 1] + imag_part * values[:, 0],
        ],
        axis=1,
    )


def combine_stats(first_pair, second_pair):
    return (jnp.maximum(first_pair[0], second_pair[0]), first_pair[1] + second_pair[1])


def per_device(traces, wavelet):
    row_count = traces.shape[2]
    col_count = traces.shape[3]
    extent = row_count * lax.axis_size(SRC)
    row_anchor = lax.axis_index(SRC) * row_count
    col_anchor = lax.axis_index(RCV) * col_count
    root_scale = 1.0 / math.sqrt(extent)
    wave_re = (wavelet[:, 0] * root_scale)[:, None, None]
    wave_im = (wavelet[:, 1] * root_scale)[:, None, None]
    forward_cols = table_block(0, extent, col_anchor, col_count, extent, -1.0)
    forward_rows = table_block(row_anchor, row_count, 0, extent, extent, -1.0)
    inverse_cols = table_block(0, extent, col_anchor, col_count, extent, 1.0)
    inverse_rows = table_block(row_anchor, row_count, 0, extent, extent, 1.0)
    coeffs = jnp.zeros(traces.shape, jnp.float32)
    columns_all = lax.all_gather(traces, SRC, axis=2, tiled=True)
    traces_f = traces.astype(jnp.float32)

    def column_section(table, portion):
        return complex_product(table, portion, "mn,fnc->fmc", True, False)

    def paired(first_op, second_op):
        return jnp.einsum("fmr,fkr->fmk", first_op, second_op, preferred_element_type=jnp.float32)

    norm_list = []
    for iteration in range(ITERS):
        if iteration == 0:
            misfit = traces_f
        else:
            coeff_half = coeffs.astype(jnp.bfloat16)
            halfway = column_section(
                inverse_rows, lax.all_gather(coeff_half, SRC, axis=2, tiled=True)
            ).astype(jnp.bfloat16)
            model = complex_product(
                gathered_copies(halfway, RCV, 3), inverse_cols, "fmn,nc->fmc", False, True
            ).astype(jnp.bfloat16)
            product = complex_product(
                gathered_copies(model, RCV, 3), columns_all, "fmn,fnc->fmc", False, False
            )
            misfit = traces_f - model.astype(jnp.float32) + complex_scale(wave_re, wave_im, product)
        local_squares = jnp.sum(misfit * misfit, axis=(1, 2, 3))
        misfit_half = misfit.astype(jnp.bfloat16)
        misfit_re = misfit_half[:, 0]
        misfit_im = misfit_half[:, 1]
        column_re = columns_all[:, 0]
        column_im = columns_all[:, 1]
        back_re = paired(misfit_re, column_re) + paired(misfit_im, column_re * 0 + column_im)
        back_im = paired(misfit_im, column_re) - paired(misfit_re, column_im)
        scaled = complex_scale(wave_re, -wave_im, jnp.stack([back_re, back_im], axis=1))
        embedded = lax.dynamic_update_slice(
            jnp.zeros_like(scaled), misfit_half.astype(jnp.float32), (0, 0, 0, col_anchor)
        )
        gradient_rows = lax.psum(embedded - scaled, RCV)
        halfway = complex_product(
            gradient_rows.astype(jnp.bfloat16), forward_cols, "fmn,nc->fmc", False, True
        ).astype(jnp.bfloat16)
        spectrum = column_section(forward_rows, lax.all_gather(halfway, SRC, axis=2, tiled=True))
        trial = coeffs + step_length * spectrum
        magnitude = jnp.sqrt(trial[:, 0] * trial[:, 0] + trial[:, 1] * trial[:, 1])
        local_peak = jnp.max(magnitude, axis=(1, 2))
        global_peak, total_squares = joined_all((local_peak, local_squares), SRC_RCV, combine_stats)
        norm_list.append(jnp.sqrt(total_squares))
        level = shrink_fraction * global_peak[:, None, None]
        factor = jnp.maximum(1.0 - level / jnp.maximum(magnitude, level), 0.0)
        coeffs = trial * factor[:, None]
    return (coeffs, jnp.stack(norm_list))


def solution(mesh):
    split = Mesh(mesh.devices.reshape(4, 4, 4, 2), ("src_0", "src_1", "rcv_0", "rcv_1"))
    return jax.shard_map(
        per_device,
        mesh=split,
        in_specs=(P(None, None, SRC, RCV), P()),
        out_specs=(P(None, None, SRC, RCV), P()),
        check_vma=False,
    )
```

profile of v0, /device:TPU:1, one launch (start us, length us, event | category | flops | bytes accessed | tf_op | source)
XLA Modules:
  0.0 641.2 jit_solution(3735553232752024656)
XLA Ops:
  7.2 1.7 copy.19
  10.0 2.5 broadcast.426.clone
  13.3 51.9 %all-gather.21.cloned.1.call-done = bf16[2,2,2048,256]{3,2,0,1:T(8,128)(2,1)} async-done(((bf16[2,2,128,256]{3,2,0,1:T(8,128)(2,1)}), bf16[2,2,2048,256]{3,2,0,1:T(8,128)(2,1)}) %all-gather.21.cloned.1.call-update) | async-done | bytes 4194320 | tf_op jit(solution)/shard_map/all_gather | solution.py:126
  65.3 2.5 fusion.78
  69.7 1.0 subtract_bitcast_fusion.1
  70.7 5.0 maximum_subtract_fusion
  75.7 56.5 %all-reduce.2 = bf16[2,2,128,2048]{3,2,0,1:T(8,128)(2,1)S(1)} all-reduce(f32[2,2,128,2048]{3,2,0,1:T(8,128)} %maximum_subtract_fusion), channel_id=1, replica_groups=mesh['src_0'=4,'src_1'=4,'rcv_0'=4,'rcv_1'=2] {'rcv_0','rcv_1'}, use_global_device_ids=true, to_apply=%region_0.1 | all-reduce | flops 1048576 | bytes 6291456 | tf_op jit(solution)/shard_map/psum | solution.py:163
  132.2 7.9 %fusion.62 = f32[2,128,256]{2,1,0:T(8,128)S(1)} fusion(s32[256]{0:T(256)S(1)} %iota_add_fusion, bf16[2,2,128,2048]{3,2,0,1:T(8,128)(2,1)S(1)} %all-reduce.2), kind=kOutput, calls=%fused_computation.104 | convolution fusion | flops 276824064 | bytes 1311744 | tf_op jit(solution)/shard_map/fmn,nc->fmc/dot_general | solution.py:91
  140.1 8.1 %fusion.67 = f32[2,128,256]{2,1,0:T(8,128)S(1)} fusion(s32[256]{0:T(256)S(1)} %iota_add_fusion, bf16[2,2,128,2048]{3,2,0,1:T(8,128)(2,1)S(1)} %all-reduce.2), kind=kOutput, calls=%fused_computation.106 | convolution fusion | flops 276824064 | bytes 1311744 | tf_op jit(solution)/shard_map/fmn,nc->fmc/dot_general | solution.py:91
  148.3 8.2 %fusion.44 = bf16[2,1,128,256]{3,2,0,1:T(8,128)(2,1)S(1)} fusion(f32[2,128,256]{2,1,0:T(8,128)S(1)} %fusion.62, s32[256]{0:T(256)S(1)} %iota_add_fusion, bf16[2,2,128,2048]{3,2,0,1:T(8,128)(2,1)S(1)} %all-reduce.2), kind=kOutput, calls=%fused_computation.80 | convolution fusion | flops 276955136 | bytes 1442816 | tf_op jit(solution)/shard_map/fmn,nc->fmc/dot_general | solution.py:91
  156.4 7.9 %fusion.43 = bf16[2,1,128,256]{3,2,0,1:T(8,128)(2,1)S(1)} fusion(f32[2,128,256]{2,1,0:T(8,128)S(1)} %fusion.67, s32[256]{0:T(256)S(1)} %iota_add_fusion, bf16[2,2,128,2048]{3,2,0,1:T(8,128)(2,1)S(1)} %all-reduce.2), kind=kOutput, calls=%fused_computation.79 | convolution fusion | flops 276955136 | bytes 1442816 | tf_op jit(solution)/shard_map/fmn,nc->fmc/dot_general | solution.py:91
  165.5 51.1 %all-gather.23.cloned.1.call-done = bf16[2,2,2048,256]{3,2,0,1:T(8,128)(2,1)} async-done(((bf16[2,2,128,256]{3,2,0,1:T(8,128)(2,1)}), bf16[2,2,2048,256]{3,2,0,1:T(8,128)(2,1)}) %all-gather.23.cloned.1.call-update) | async-done | bytes 4194320 | tf_op jit(solution)/shard_map/all_gather | solution.py:167
  216.7 6.0 fusion.8
  222.7 4.3 fusion.7
  227.0 4.5 fusion.26
  231.5 4.3 fusion.28
  236.0 7.6 %all-gather.8 = f32[4,2,2]{2,1,0:T(2,128)S(1)} all-gather(f32[1,2,2]{2,1,0:T(2,128)S(1)} %maximum_bitcast_fusion.1), channel_id=2, replica_groups=mesh['src_0'=4,'src_1'=4,'rcv_0'=4,'rcv_1'=2] {'src_0'}, dimensions={0}, use_global_device_ids=true | all-gather | bytes 80 | tf_op jit(solution)/shard_map/all_gather | solution.py:39
  243.7 5.9 all-gather.9
  249.6 7.8 %all-gather.10 = f32[4,2,2]{2,1,0:T(2,128)S(1)} all-gather(f32[1,2,2]{2,1,0:T(2,128)S(1)} %maximum_bitcast_fusion.3), channel_id=4, replica_groups=mesh['src_0'=4,'src_1'=4,'rcv_0'=4,'rcv_1'=2] {'rcv_0'}, dimensions={0}, use_global_device_ids=true | all-gather | bytes 80 | tf_op jit(solution)/shard_map/all_gather | solution.py:39
  257.4 8.2 %all-gather.11 = f32[2,2,2]{2,1,0:T(2,128)S(1)} all-gather(f32[1,2,2]{2,1,0:T(2,128)S(1)} %maximum_bitcast_fusion.4), channel_id=5, replica_groups=mesh['src_0'=4,'src_1'=4,'rcv_0'=4,'rcv_1'=2] {'rcv_1'}, dimensions={0}, use_global_device_ids=true | all-gather | bytes 48 | tf_op jit(solution)/shard_map/all_gather | solution.py:39
  267.0 50.0 %all-gather.25.cloned.1.call-done = bf16[2,2,2048,256]{2,3,0,1:T(8,128)(2,1)} async-done(((bf16[2,2,128,256]{2,3,0,1:T(8,128)(2,1)}), bf16[2,2,2048,256]{2,3,0,1:T(8,128)(2,1)}) %all-gather.25.cloned.1.call-update) | async-done | bytes 4194320 | tf_op jit(solution)/shard_map/all_gather | solution.py:142
  317.0 6.1 fusion.12
  323.1 4.4 fusion.11
  327.5 4.6 fusion.37
  332.1 4.4 fusion.38
  336.9 32.3 %all_to_all.10 = bf16[8,2,2,128,256]{4,3,1,2,0:T(8,128)(2,1)S(1)} all-to-all(bf16[8,2,2,128,256]{4,3,1,2,0:T(8,128)(2,1)S(1)} %broadcast_in_dim.4), channel_id=1, replica_groups=mesh['src_0'=4,'src_1'=4,'rcv_0'=4,'rcv_1'=2] {'rcv_0','rcv_1'}, dimensions={0} | all-to-all | bytes 4194304 | tf_op jit(solution)/shard_map/all_to_all | solution.py:24
  369.5 7.9 %fusion.59 = f32[2,128,256]{2,1,0:T(8,128)S(1)} fusion(s32[256]{0:T(256)S(1)} %iota_add_fusion, bf16[2,2,128,2048]{3,2,0,1:T(8,128)(2,1)S(1)} %bitcast.296), kind=kOutput, calls=%fused_computation.103 | convolution fusion | flops 276824064 | bytes 1311744 | tf_op jit(solution)/shard_map/fmn,nc->fmc/dot_general | solution.py:91
  377.4 8.3 %fusion.70 = f32[2,128,256]{2,1,0:T(8,128)S(1)} fusion(s32[256]{0:T(256)S(1)} %iota_add_fusion, bf16[2,2,128,2048]{3,2,0,1:T(8,128)(2,1)S(1)} %bitcast.297), kind=kOutput, calls=%fused_computation.107 | convolution fusion | flops 276824064 | bytes 1311744 | tf_op jit(solution)/shard_map/fmn,nc->fmc/dot_general | solution.py:91
  385.7 8.1 %fusion.42 = bf16[2,1,128,256]{3,2,0,1:T(8,128)(2,1)S(1)} fusion(f32[2,128,256]{2,1,0:T(8,128)S(1)} %fusion.59, s32[256]{0:T(256)S(1)} %iota_add_fusion, bf16[2,2,128,2048]{3,2,0,1:T(8,128)(2,1)S(1)} %bitcast.298), kind=kOutput, calls=%fused_computation.78 | convolution fusion | flops 276955136 | bytes 1442816 | tf_op jit(solution)/shard_map/fmn,nc->fmc/dot_general | solution.py:91
  393.9 7.9 %fusion.41 = bf16[2,1,128,256]{3,2,0,1:T(8,128)(2,1)S(1)} fusion(f32[2,128,256]{2,1,0:T(8,128)S(1)} %fusion.70, s32[256]{0:T(256)S(1)} %iota_add_fusion, bf16[2,2,128,2048]{3,2,0,1:T(8,128)(2,1)S(1)} %bitcast.299), kind=kOutput, calls=%fused_computation.77 | convolution fusion | flops 276955136 | bytes 1442816 | tf_op jit(solution)/shard_map/fmn,nc->fmc/dot_general | solution.py:91
  402.0 29.7 %all_to_all.11 = bf16[8,2,2,128,256]{4,3,1,2,0:T(8,128)(2,1)S(1)} all-to-all(bf16[8,2,2,128,256]{4,3,1,2,0:T(8,128)(2,1)S(1)} %broadcast_in_dim.5), channel_id=1, replica_groups=mesh['src_0'=4,'src_1'=4,'rcv_0'=4,'rcv_1'=2] {'rcv_0','rcv_1'}, dimensions={0} | all-to-all | bytes 4194304 | tf_op jit(solution)/shard_map/all_to_all | solution.py:24
  432.0 1.9 copy-done.1
  439.9 2.7 maximum_subtract_fusion.1
  442.6 56.6 %all-reduce.3 = bf16[2,2,128,2048]{3,2,0,1:T(8,128)(2,1)S(1)} all-reduce(f32[2,2,128,2048]{3,2,0,1:T(8,128)} %maximum_subtract_fusion.1), channel_id=1, replica_groups=mesh['src_0'=4,'src_1'=4,'rcv_0'=4,'rcv_1'=2] {'rcv_0','rcv_1'}, use_global_device_ids=true, to_apply=%region_3.4 | all-reduce | flops 1048576 | bytes 6291456 | tf_op jit(solution)/shard_map/psum | solution.py:163
  499.2 7.9 %fusion.56 = f32[2,128,256]{2,1,0:T(8,128)S(1)} fusion(s32[256]{0:T(256)S(1)} %iota_add_fusion, bf16[2,2,128,2048]{3,2,0,1:T(8,128)(2,1)S(1)} %all-reduce.3), kind=kOutput, calls=%fused_computation.102 | convolution fusion | flops 276824064 | bytes 1311744 | tf_op jit(solution)/shard_map/fmn,nc->fmc/dot_general | solution.py:91
  507.1 8.1 %fusion.64 = f32[2,128,256]{2,1,0:T(8,128)S(1)} fusion(s32[256]{0:T(256)S(1)} %iota_add_fusion, bf16[2,2,128,2048]{3,2,0,1:T(8,128)(2,1)S(1)} %all-reduce.3), kind=kOutput, calls=%fused_computation.105 | convolution fusion | flops 276824064 | bytes 1311744 | tf_op jit(solution)/shard_map/fmn,nc->fmc/dot_general | solution.py:91
  515.2 8.2 %fusion.40 = bf16[2,1,128,256]{3,2,0,1:T(8,128)(2,1)S(1)} fusion(f32[2,128,256]{2,1,0:T(8,128)S(1)} %fusion.56, s32[256]{0:T(256)S(1)} %iota_add_fusion, bf16[2,2,128,2048]{3,2,0,1:T(8,128)(2,1)S(1)} %all-reduce.3), kind=kOutput, calls=%fused_computation.76 | convolution fusion | flops 276955136 | bytes 1442816 | tf_op jit(solution)/shard_map/fmn,nc->fmc/dot_general | solution.py:91
  523.4 7.9 %fusion.39 = bf16[2,1,128,256]{3,2,0,1:T(8,128)(2,1)S(1)} fusion(f32[2,128,256]{2,1,0:T(8,128)S(1)} %fusion.64, s32[256]{0:T(256)S(1)} %iota_add_fusion, bf16[2,2,128,2048]{3,2,0,1:T(8,128)(2,1)S(1)} %all-reduce.3), kind=kOutput, calls=%fused_computation.75 | convolution fusion | flops 276955136 | bytes 1442816 | tf_op jit(solution)/shard_map/fmn,nc->fmc/dot_general | solution.py:91
  532.0 51.3 %all-gather.27.cloned.1.call-done = bf16[2,2,2048,256]{3,2,0,1:T(8,128)(2,1)} async-done(((bf16[2,2,128,256]{3,2,0,1:T(8,128)(2,1)}), bf16[2,2,2048,256]{3,2,0,1:T(8,128)(2,1)}) %all-gather.27.cloned.1.call-update) | async-done | bytes 4194320 | tf_op jit(solution)/shard_map/all_gather | solution.py:167
  583.3 6.4 fusion.16
  589.7 4.3 fusion.15
  594.0 4.3 fusion.20
  598.3 4.5 fusion.22
  603.1 7.6 %all-gather.12 = f32[4,2,2]{2,1,0:T(2,128)S(1)} all-gather(f32[1,2,2]{2,1,0:T(2,128)S(1)} %maximum_bitcast_fusion.5), channel_id=6, replica_groups=mesh['src_0'=4,'src_1'=4,'rcv_0'=4,'rcv_1'=2] {'src_0'}, dimensions={0}, use_global_device_ids=true | all-gather | bytes 80 | tf_op jit(solution)/shard_map/all_gather | solution.py:39
  610.8 5.9 all-gather.13
  616.7 7.8 %all-gather.14 = f32[4,2,2]{2,1,0:T(2,128)S(1)} all-gather(f32[1,2,2]{2,1,0:T(2,128)S(1)} %maximum_bitcast_fusion.7), channel_id=8, replica_groups=mesh['src_0'=4,'src_1'=4,'rcv_0'=4,'rcv_1'=2] {'rcv_0'}, dimensions={0}, use_global_device_ids=true | all-gather | bytes 80 | tf_op jit(solution)/shard_map/all_gather | solution.py:39
  624.5 8.2 %all-gather.15 = f32[2,2,2]{2,1,0:T(2,128)S(1)} all-gather(f32[1,2,2]{2,1,0:T(2,128)S(1)} %maximum_bitcast_fusion.8), channel_id=9, replica_groups=mesh['src_0'=4,'src_1'=4,'rcv_0'=4,'rcv_1'=2] {'rcv_1'}, dimensions={0}, use_global_device_ids=true | all-gather | bytes 48 | tf_op jit(solution)/shard_map/all_gather | solution.py:39
  633.0 1.0 copy.35
  (70 shorter events, 15.9 us)
Async XLA Ops:
  7.2 58.1 %all-gather.21.cloned.1.call-start = ((), (), s32[]{:S(2)}) async-start(), calls=%async_computation.2 | async-start | bytes 4456448 | tf_op jit(solution)/shard_map/all_gather | solution.py:126
  8.9 207.7 %all-gather.23.cloned.1.call-start = ((), (), s32[]{:S(2)}) async-start(), calls=%async_computation.3 | async-start | bytes 4456448 | tf_op jit(solution)/shard_map/all_gather | solution.py:167
  10.0 2.5 copy-start.2
  65.3 2.8 copy-start
  165.1 151.9 %all-gather.25.cloned.1.call-start = ((), (), s32[]{:S(2)}) async-start(), calls=%async_computation.4 | async-start | bytes 4456448 | tf_op jit(solution)/shard_map/all_gather | solution.py:142
  216.7 6.0 copy-start.3
  266.5 316.8 %all-gather.27.cloned.1.call-start = ((), (), s32[]{:S(2)}) async-start(), calls=%async_computation.5 | async-start | bytes 4456448 | tf_op jit(solution)/shard_map/all_gather | solution.py:167
  317.0 6.1 copy-start.4
  431.7 2.2 copy-start.1
  583.3 6.4 %copy-start.5 = (bf16[2,2,2048,256]{3,2,0,1:T(8,128)(2,1)S(1)}, bf16[2,2,2048,256]{3,2,0,1:T(8,128)(2,1)}, u32[]{:S(2)}) copy-start(bf16[2,2,2048,256]{3,2,0,1:T(8,128)(2,1)} %all-gather.27.cloned.1.call-done) | copy-start | bytes 12582916
Sparse Core Ops, SparseCore 0:
  10.7 54.5 all-gather.20
  165.2 51.4 all-gather.22
  266.6 50.2 all-gather.24
  532.2 51.0 all-gather.26
where the time goes:
time: 645 us; the launch traced here: 641 us
  blocking collectives  234 us (36%)
  waiting for transfers between devices  204 us (32%)
  matrix products  165 us (26%)
  between operations  14.4 us (2%)
  other arithmetic  13.8 us (2%)
  local copies, waits for them, and re-layouts  9 us (1%)
    dot_general x28, matrix products, single(): jnp.einsum(pattern, first_op, second_op, preferred_element_type=jnp.float32)  156 us
    psum x2, blocking collectives, per_device(): gradient_rows = lax.psum(embedded - scaled, RCV)  113 us
    all_gather x2, waiting for transfers between devices, per_device(): lax.all_gather(halfway, SRC, axis=2, tiled=True)  102 us
    all_to_all x2, blocking collectives, copy_for_each(): return lax.all_to_all(copies, axis, split_axis=0, concat_axis=0, tiled=True)  61.9 us
    all_gather x8, blocking collectives, all_in_one(): both, at, found = (lax.all_gather(jnp.concatenate(lines), axis), 0, {})  59 us
    all_gather x1, waiting for transfers between devices, per_device(): columns_all = lax.all_gather(traces, SRC, axis=2, tiled=True)  51.9 us
    all_gather x1, waiting for transfers between devices, per_device(): lax.all_gather(coeff_half, SRC, axis=2, tiled=True)  50 us
  transfers between devices with their start and end apart: 4, of which 4 were waited for; matrix products, arithmetic and copies ran while one was open for 1% of the time, Pallas kernels for 0%

commit v1 on v0

--- a/solution.py
+++ b/solution.py
@@ -160,7 +160,7 @@
         embedded = lax.dynamic_update_slice(
             jnp.zeros_like(scaled), misfit_half.astype(jnp.float32), (0, 0, 0, col_anchor)
         )
-        gradient_rows = lax.psum(embedded - scaled, RCV)
+        gradient_rows = jnp.sum(lax.all_gather(embedded - scaled, RCV), axis=0)
         halfway = complex_product(
             gradient_rows.astype(jnp.bfloat16), forward_cols, "fmn,nc->fmc", False, True
         ).astype(jnp.bfloat16)

time: 645 us -> 870 us (1.35)
  waiting for transfers between devices: 204 us -> 516 us
  blocking collectives: 234 us -> 121 us
  other arithmetic: 13.8 us -> 39.7 us
    all_gather x0 -> x2, waiting for transfers between devices: none -> 310 us  [per_device(): gradient_rows = jnp.sum(lax.all_gather(embedded - scaled, RCV), axis=0)]
    psum x2 -> x0, blocking collectives: 113 us -> none  [per_device(): gradient_rows = lax.psum(embedded - scaled, RCV)]
    reduce_sum x0 -> x2, other arithmetic: none -> 25.8 us  [per_device(): gradient_rows = jnp.sum(lax.all_gather(embedded - scaled, RCV), axis=0)]
  transfers between devices with their start and end apart: 4 -> 6, of which waited for: 4 -> 6; matrix products, arithmetic and copies ran while one was open for 1% -> 0% of each run, Pallas kernels for 0% -> 0%
where the time goes in v1:
time: 870 us; the launch traced here: 866 us
  waiting for transfers between devices  516 us (59%)
  matrix products  165 us (19%)
  blocking collectives  121 us (14%)
  other arithmetic  39.7 us (5%)
  between operations  14.7 us (2%)
  local copies, waits for them, and re-layouts  8.96 us (1%)
    all_gather x2, waiting for transfers between devices, per_device(): gradient_rows = jnp.sum(lax.all_gather(embedded - scaled, RCV), axis=0)  310 us
    dot_general x28, matrix products, single(): jnp.einsum(pattern, first_op, second_op, preferred_element_type=jnp.float32)  156 us
    all_gather x2, waiting for transfers between devices, per_device(): lax.all_gather(halfway, SRC, axis=2, tiled=True)  104 us
    all_to_all x2, blocking collectives, copy_for_each(): return lax.all_to_all(copies, axis, split_axis=0, concat_axis=0, tiled=True)  61.9 us
    all_gather x8, blocking collectives, all_in_one(): both, at, found = (lax.all_gather(jnp.concatenate(lines), axis), 0, {})  59 us
    all_gather x1, waiting for transfers between devices, per_device(): columns_all = lax.all_gather(traces, SRC, axis=2, tiled=True)  51.9 us
    all_gather x1, waiting for transfers between devices, per_device(): lax.all_gather(coeff_half, SRC, axis=2, tiled=True)  50 us
    reduce_sum x2, other arithmetic, per_device(): gradient_rows = jnp.sum(lax.all_gather(embedded - scaled, RCV), axis=0)  25.8 us
  transfers between devices with their start and end apart: 6, of which 6 were waited for; matrix products, arithmetic and copies ran while one was open for 0% of the time, Pallas kernels for 0%

profile of v1, /device:TPU:1, one launch (start us, length us, event | category | flops | bytes accessed | tf_op | source)
XLA Modules:
  0.0 866.1 jit_solution(16160079391879457118)
XLA Ops:
  7.2 1.7 copy.19
  10.0 2.5 broadcast.426.clone
  13.3 51.9 %all-gather.25.cloned.1.call-done = bf16[2,2,2048,256]{3,2,0,1:T(8,128)(2,1)} async-done(((bf16[2,2,128,256]{3,2,0,1:T(8,128)(2,1)}), bf16[2,2,2048,256]{3,2,0,1:T(8,128)(2,1)}) %all-gather.25.cloned.1.call-update) | async-done | bytes 4194320 | tf_op jit(solution)/shard_map/all_gather | solution.py:126
  65.3 2.5 fusion.78
  70.7 5.0 maximum_subtract_fusion
  75.8 156.1 %all-gather.33.cloned.1.call-done = f32[16,2,128,2048]{3,2,0,1:T(8,128)} async-done(((f32[2,2,128,2048]{3,2,0,1:T(8,128)}), f32[16,2,128,2048]{3,2,0,1:T(8,128)}) %all-gather.33.cloned.1.call-update) | async-done | bytes 33554448 | tf_op jit(solution)/shard_map/all_gather | solution.py:163
  231.9 12.9 %reduce_sum.36 = bf16[2,2,128,2048]{3,2,0,1:T(8,128)(2,1)S(1)} reduce(f32[8,2,2,128,2048]{4,3,1,0,2:T(8,128)} %bitcast.292, f32[]{:T(128)} %constant.28.clone.1), dimensions={0}, to_apply=%region_0.1 | reduce | flops 7340032 | bytes 35651588 | tf_op jit(solution)/shard_map/reduce_sum | solution.py:163
  244.9 7.9 fusion.62
  252.8 8.1 fusion.67
  260.9 8.2 fusion.44
  269.1 7.9 fusion.43
  278.2 51.6 %all-gather.27.cloned.1.call-done = bf16[2,2,2048,256]{3,2,0,1:T(8,128)(2,1)} async-done(((bf16[2,2,128,256]{3,2,0,1:T(8,128)(2,1)}), bf16[2,2,2048,256]{3,2,0,1:T(8,128)(2,1)}) %all-gather.27.cloned.1.call-update) | async-done | bytes 4194320 | tf_op jit(solution)/shard_map/all_gather | solution.py:167
  329.8 6.0 fusion.8
  335.8 4.3 fusion.7
  340.1 4.5 fusion.26
  344.6 4.3 fusion.28
  349.1 7.6 all-gather.10
  356.8 5.9 all-gather.11
  362.7 7.8 all-gather.12
  370.5 8.2 all-gather.13
  380.1 50.0 %all-gather.29.cloned.1.call-done = bf16[2,2,2048,256]{2,3,0,1:T(8,128)(2,1)} async-done(((bf16[2,2,128,256]{2,3,0,1:T(8,128)(2,1)}), bf16[2,2,2048,256]{2,3,0,1:T(8,128)(2,1)}) %all-gather.29.cloned.1.call-update) | async-done | bytes 4194320 | tf_op jit(solution)/shard_map/all_gather | solution.py:142
  430.1 6.1 fusion.12
  436.2 4.4 fusion.11
  440.6 4.6 fusion.37
  445.2 4.4 fusion.38
  450.0 32.3 %all_to_all.10 = bf16[8,2,2,128,256]{4,3,1,2,0:T(8,128)(2,1)S(1)} all-to-all(bf16[8,2,2,128,256]{4,3,1,2,0:T(8,128)(2,1)S(1)} %broadcast_in_dim.4), channel_id=1, replica_groups=mesh['src_0'=4,'src_1'=4,'rcv_0'=4,'rcv_1'=2] {'rcv_0','rcv_1'}, dimensions={0} | all-to-all | bytes 4194304 | tf_op jit(solution)/shard_map/all_to_all | solution.py:24
  482.6 7.9 fusion.59
  490.5 8.3 fusion.70
  498.8 8.1 fusion.42
  507.0 7.9 fusion.41
  515.1 29.7 %all_to_all.11 = bf16[8,2,2,128,256]{4,3,1,2,0:T(8,128)(2,1)S(1)} all-to-all(bf16[8,2,2,128,256]{4,3,1,2,0:T(8,128)(2,1)S(1)} %broadcast_in_dim.5), channel_id=1, replica_groups=mesh['src_0'=4,'src_1'=4,'rcv_0'=4,'rcv_1'=2] {'rcv_0','rcv_1'}, dimensions={0} | all-to-all | bytes 4194304 | tf_op jit(solution)/shard_map/all_to_all | solution.py:24
  545.1 1.9 copy-done.1
  553.1 2.8 maximum_subtract_fusion.1
  556.0 154.2 %all-gather.35.cloned.1.call-done = f32[16,2,128,2048]{3,2,0,1:T(8,128)} async-done(((f32[2,2,128,2048]{3,2,0,1:T(8,128)}), f32[16,2,128,2048]{3,2,0,1:T(8,128)}) %all-gather.35.cloned.1.call-update) | async-done | bytes 33554448 | tf_op jit(solution)/shard_map/all_gather | solution.py:163
  710.1 12.8 %reduce_sum.38 = bf16[2,2,128,2048]{3,2,0,1:T(8,128)(2,1)S(1)} reduce(f32[8,2,2,128,2048]{4,3,1,0,2:T(8,128)} %bitcast.293, f32[]{:T(128)} %constant.28.clone.1), dimensions={0}, to_apply=%region_3.4 | reduce | flops 7340032 | bytes 35651588 | tf_op jit(solution)/shard_map/reduce_sum | solution.py:163
  722.9 7.9 fusion.56
  730.8 8.1 fusion.64
  739.0 8.2 fusion.40
  747.1 7.9 fusion.39
  755.8 52.0 %all-gather.31.cloned.1.call-done = bf16[2,2,2048,256]{3,2,0,1:T(8,128)(2,1)} async-done(((bf16[2,2,128,256]{3,2,0,1:T(8,128)(2,1)}), bf16[2,2,2048,256]{3,2,0,1:T(8,128)(2,1)}) %all-gather.31.cloned.1.call-update) | async-done | bytes 4194320 | tf_op jit(solution)/shard_map/all_gather | solution.py:167
  807.8 6.4 fusion.16
  814.2 4.3 fusion.15
  818.6 4.3 fusion.20
  822.9 4.4 fusion.22
  827.6 7.6 all-gather.14
  835.3 5.9 all-gather.15
  841.2 7.8 all-gather.16
  849.0 8.2 all-gather.17
  (76 shorter events, 18.0 us)
Async XLA Ops:
  7.2 58.1 %all-gather.25.cloned.1.call-start = ((), (), s32[]{:S(2)}) async-start(), calls=%async_computation.2 | async-start | bytes 4456448 | tf_op jit(solution)/shard_map/all_gather | solution.py:126
  8.9 223.0 %all-gather.33.cloned.1.call-start = ((), (), s32[]{:S(2)}) async-start(), calls=%async_computation.6 | async-start | bytes 37748736 | tf_op jit(solution)/shard_map/all_gather | solution.py:163
  9.9 2.5 copy-start.2
  65.3 2.8 copy-start
  75.8 254.0 %all-gather.27.cloned.1.call-start = ((), (), s32[]{:S(2)}) async-start(), calls=%async_computation.3 | async-start | bytes 4456448 | tf_op jit(solution)/shard_map/all_gather | solution.py:167
  277.7 152.3 %all-gather.29.cloned.1.call-start = ((), (), s32[]{:S(2)}) async-start(), calls=%async_computation.4 | async-start | bytes 4456448 | tf_op jit(solution)/shard_map/all_gather | solution.py:142
  329.8 6.0 copy-start.3
  379.6 330.5 %all-gather.35.cloned.1.call-start = ((), (), s32[]{:S(2)}) async-start(), calls=%async_computation.7 | async-start | bytes 37748736 | tf_op jit(solution)/shard_map/all_gather | solution.py:163
  430.1 6.1 copy-start.4
  544.8 2.2 copy-start.1
  555.9 251.9 %all-gather.31.cloned.1.call-start = ((), (), s32[]{:S(2)}) async-start(), calls=%async_computation.5 | async-start | bytes 4456448 | tf_op jit(solution)/shard_map/all_gather | solution.py:167
  807.8 6.4 copy-start.5
Sparse Core Ops, SparseCore 0:
  10.7 54.5 all-gather.24
  75.9 156.0 all-gather.32
  277.9 51.8 all-gather.26
  379.8 50.2 all-gather.28
  556.0 154.0 all-gather.34
  755.9 51.8 all-gather.30
